TPU v7x, 8 devices: a whole 2x2x1 slice. The times are simulated.
8 devices in a mesh: batch: 1 (over z), row: 2 (over y), col: 4 (over x, core).
Axes of the slice: x: 2, y: 2, z: 1, core: 2. Of those that a mesh axis runs over, the one named last changes fastest.
Arguments:
- spd_blocks: float32 [64, 128, 8192], P(('batch', 'row'), None, 'col')
Outputs:
- output: float32 [64, 128, 8192], P(('batch', 'row'), None, 'col')
All inputs are finite; a program needn't handle non-finite values.
Results may differ from a plain program's by a relative error of at most 0.001.
Values are sent between devices in bfloat16 or wider.
A program may use at most 1 GiB of HBM per device.

v0:
```python
import functools
import jax
import jax.numpy as jnp
from jax import lax
from jax.sharding import PartitionSpec as P, NamedSharding


def transposed_panel(row_panel, row_id, col_id, row_devs, col_devs, row_skip, col_skip):
    row_blocks = row_panel.shape[0]
    blk_size = row_panel.shape[1]
    if row_devs >= col_devs:
        grid_ratio = row_devs // col_devs
        blk_shift = (row_skip * row_devs - col_skip * col_devs) // col_devs
        pick_mask = (jnp.arange(grid_ratio) == row_id // col_devs) & (row_id % col_devs == col_id)
        spread = (row_panel[:, None] * pick_mask.astype(jnp.bfloat16)[None, :, None, None]).reshape(row_blocks * grid_ratio, blk_size, blk_size)
        if blk_shift >= 0:
            spread = jnp.pad(spread, ((blk_shift, 0), (0, 0), (0, 0)))
        else:
            spread = spread[-blk_shift:]
    else:
        grid_ratio = col_devs // row_devs
        blk_shift = (col_skip * col_devs - row_skip * row_devs) // row_devs
        if blk_shift >= 0:
            shifted = row_panel[blk_shift:]
        else:
            shifted = jnp.pad(row_panel, ((-blk_shift, 0), (0, 0), (0, 0)))
        grouped = shifted.reshape(shifted.shape[0] // grid_ratio, grid_ratio, blk_size, blk_size)
        chosen = lax.dynamic_index_in_dim(grouped, col_id // row_devs, axis=1, keepdims=False)
        spread = jnp.where(row_id == col_id % row_devs, chosen, jnp.zeros_like(chosen))
    return lax.psum(spread, "row")


def solution(mesh):
    row_devs = mesh.shape["row"]
    col_devs = mesh.shape["col"]

    def factor_local(a_loc):
        row_blocks, blk_size, local_cols = a_loc.shape
        col_blocks = local_cols // blk_size
        blk_count = row_blocks * row_devs
        row_id = lax.axis_index("row")
        col_id = lax.axis_index("col")
        eye_blk = jnp.eye(blk_size, dtype=jnp.float32)

        def panel_step(step_idx, window):
            win_rows, win_cols = window.shape
            win_rblk = win_rows // blk_size
            row_skip = row_blocks - win_rblk
            col_skip = col_blocks - win_cols // blk_size
            own_col = col_id == step_idx % col_devs
            is_owner = own_col & (row_id == step_idx % row_devs)
            col_off = (step_idx // col_devs - col_skip) * blk_size
            col_blk = lax.dynamic_slice_in_dim(window, col_off, blk_size, axis=1)
            diag_blk = lax.dynamic_slice_in_dim(col_blk, (step_idx // row_devs - row_skip) * blk_size, blk_size, axis=0)
            diag_own = jnp.tril(jnp.linalg.cholesky(jnp.where(is_owner, diag_blk, eye_blk)))
            diag_fac = lax.psum(jnp.where(is_owner, diag_own, 0.0), "row")
            diag_fac = jnp.where(own_col, diag_fac, eye_blk)
            solved = lax.linalg.triangular_solve(diag_fac, col_blk, left_side=False, lower=True, transpose_a=True)
            row_ids = (row_skip + jnp.arange(win_rblk)) * row_devs + row_id
            below_mask = (row_ids > step_idx)[:, None, None]
            on_diag = (row_ids == step_idx)[:, None, None]
            solved_blocks = solved.reshape(win_rblk, blk_size, blk_size)
            prior_col = col_blk.reshape(win_rblk, blk_size, blk_size)
            new_col = jnp.where(below_mask, solved_blocks, jnp.where(on_diag, diag_fac[None], prior_col))
            new_col = jnp.where(own_col, new_col, prior_col).reshape(win_rows, blk_size)
            window = lax.dynamic_update_slice_in_dim(window, new_col, col_off, axis=1)
            row_panel = lax.psum(jnp.where(below_mask & own_col, solved_blocks, 0.0).astype(jnp.bfloat16), "col")
            col_panel = transposed_panel(row_panel, row_id, col_id, row_devs, col_devs, row_skip, col_skip)
            update = lax.dot_general(row_panel.reshape(win_rows, blk_size), col_panel.reshape(win_cols, blk_size), (((1,), (1,)), ((), ())), preferred_element_type=jnp.float32)
            return window - update

        work_mat = a_loc.reshape(row_blocks * blk_size, local_cols)
        phase_count = min(blk_count, 8)
        bounds = [(phase_idx * blk_count) // phase_count for phase_idx in range(phase_count + 1)]
        for phase_idx in range(phase_count):
            row_start = (bounds[phase_idx] // row_devs) * blk_size
            col_start = (bounds[phase_idx] // col_devs) * blk_size
            window = lax.fori_loop(bounds[phase_idx], bounds[phase_idx + 1], panel_step, work_mat[row_start:, col_start:])
            work_mat = lax.dynamic_update_slice(work_mat, window, (row_start, col_start))
        row_blk_ids = jnp.arange(row_blocks) * row_devs + row_id
        col_blk_ids = jnp.arange(col_blocks) * col_devs + col_id
        keep_mask = row_blk_ids[:, None, None, None] >= col_blk_ids[None, None, :, None]
        factor = jnp.where(keep_mask, work_mat.reshape(row_blocks, blk_size, col_blocks, blk_size), 0.0)
        return factor.reshape(row_blocks, blk_size, local_cols)

    blk_spec = P(("batch", "row"), None, "col")
    return jax.shard_map(factor_local, mesh=mesh, in_specs=(blk_spec,), out_specs=blk_spec, check_vma=False)
```

profile of v0, /device:TPU:0, one launch (start us, length us, event | category | flops | bytes accessed | tf_op | source)
XLA Modules:
  0.0 6844.2 jit_solution(1766057538012142098)
XLA Ops:
  29.7 1030.0 %while.152 = (s32[]{:T(128)}, f32[4096,2048]{1,0:T(8,128)}, s32[]{:T(128)}, s32[]{:T(128)}, pred[]{:T(512)}, /*index=5*/s32[]{:T(128)}, s32[]{:T(128)}, s32[]{:T...) while((s32[]{:T(128)}, f32[4096,2048]{1,0:T(8,128)}, ...), condition=%wide.region_6.8_spmd.clone.clone, body=%wide.region_0.7_spmd.clone.clone.sunk | while | flops 2965209344 | bytes 96405352 | solution.py:78
  80.1 30.1 all-reduce.27.cloned.1.call-done
  207.5 30.9 all-reduce.27.cloned.1.call-done
  335.7 31.7 all-reduce.27.cloned.1.call-done
  464.8 30.9 all-reduce.27.cloned.1.call-done
  593.7 30.1 all-reduce.27.cloned.1.call-done
  721.0 30.9 all-reduce.27.cloned.1.call-done
  849.1 31.8 all-reduce.27.cloned.1.call-done
  978.3 30.9 all-reduce.27.cloned.1.call-done
  1076.8 968.4 %while.153 = (s32[]{:T(128)}, f32[3584,1792]{1,0:T(8,128)}, s32[]{:T(128)}, s32[]{:T(128)}, pred[]{:T(512)}, /*index=5*/s32[]{:T(128)}, s32[]{:T(128)}, s32[]{:T...) while((s32[]{:T(128)}, f32[3584,1792]{1,0:T(8,128)}, ...), condition=%wide.region_11.13_spmd.clone.clone, body=%wide.region_7.12_spmd.clone.clone.sunk | while | flops 2358804736 | bytes 77203448 | solution.py:78
  1124.5 29.4 all-reduce.33.cloned.1.call-done
  1244.4 30.3 all-reduce.33.cloned.1.call-done
  1365.1 31.1 all-reduce.33.cloned.1.call-done
  1486.7 30.2 all-reduce.33.cloned.1.call-done
  1608.3 29.4 all-reduce.33.cloned.1.call-done
  1728.2 30.3 all-reduce.33.cloned.1.call-done
  1849.1 31.1 all-reduce.33.cloned.1.call-done
  1970.7 30.3 all-reduce.33.cloned.1.call-done
  2079.2 892.7 %while.154 = (s32[]{:T(128)}, f32[3072,1536]{1,0:T(8,128)}, s32[]{:T(128)}, s32[]{:T(128)}, pred[]{:T(512)}, /*index=5*/s32[]{:T(128)}, s32[]{:T(128)}, s32[]{:T...) while((s32[]{:T(128)}, f32[3072,1536]{1,0:T(8,128)}, ...), condition=%wide.region_16.18_spmd.clone.clone, body=%wide.region_12.17_spmd.clone.clone.sunk | while | flops 1819771136 | bytes 60098532 | solution.py:78
  2123.9 28.6 all-reduce.39.cloned.1.call-done
  2234.4 29.5 all-reduce.39.cloned.1.call-done
  2345.8 30.3 all-reduce.39.cloned.1.call-done
  2458.1 29.5 all-reduce.39.cloned.1.call-done
  2570.4 28.6 all-reduce.39.cloned.1.call-done
  2680.9 29.5 all-reduce.39.cloned.1.call-done
  2792.2 30.3 all-reduce.39.cloned.1.call-done
  2904.5 29.5 all-reduce.39.cloned.1.call-done
  2995.0 838.9 %while.155 = (s32[]{:T(128)}, f32[2560,1280]{1,0:T(8,128)}, s32[]{:T(128)}, s32[]{:T(128)}, pred[]{:T(512)}, /*index=5*/s32[]{:T(128)}, s32[]{:T(128)}, s32[]{:T...) while((s32[]{:T(128)}, f32[2560,1280]{1,0:T(8,128)}, ...), condition=%wide.region_21.23_spmd.clone.clone, body=%wide.region_17.22_spmd.clone.clone.sunk | while | flops 1348108544 | bytes 45090764 | solution.py:78
  3143.3 28.3 all-reduce.45.cloned.1.call-done
  3248.0 29.2 all-reduce.45.cloned.1.call-done
  3353.5 28.3 all-reduce.45.cloned.1.call-done
  3562.5 28.3 all-reduce.45.cloned.1.call-done
  3667.2 29.2 all-reduce.45.cloned.1.call-done
  3772.5 28.3 all-reduce.45.cloned.1.call-done
  3852.7 793.4 %while.156 = (s32[]{:T(128)}, f32[2048,1024]{1,0:T(8,128)}, s32[]{:T(128)}, s32[]{:T(128)}, pred[]{:T(512)}, /*index=5*/s32[]{:T(128)}, s32[]{:T(128)}, s32[]{:T...) while((s32[]{:T(128)}, f32[2048,1024]{1,0:T(8,128)}, ...), condition=%wide.region_26.28_spmd.clone.clone, body=%wide.region_22.27_spmd.clone.clone.sunk | while | flops 943816960 | bytes 32180148 | solution.py:78
  3994.8 27.8 all-reduce.51.cloned.1.call-done
  4093.8 28.7 all-reduce.51.cloned.1.call-done
  4193.5 27.8 all-reduce.51.cloned.1.call-done
  4391.5 27.8 all-reduce.51.cloned.1.call-done
  4490.5 28.7 all-reduce.51.cloned.1.call-done
  4590.2 27.8 all-reduce.51.cloned.1.call-done
  4659.3 757.7 %while.157 = (s32[]{:T(128)}, f32[1536,768]{1,0:T(8,128)}, s32[]{:T(128)}, s32[]{:T(128)}, pred[]{:T(512)}, /*index=5*/s32[]{:T(128)}, s32[]{:T(128)}, s32[]{:T(...) while((s32[]{:T(128)}, f32[1536,768]{1,0:T(8,128)}, ...), condition=%wide.region_31.33_spmd.clone.clone, body=%wide.region_27.32_spmd.clone.clone.sunk | while | flops 606896384 | bytes 21366684 | solution.py:78
  4891.5 28.0 all-reduce.57.cloned.1.call-done
  5270.3 28.0 all-reduce.57.cloned.1.call-done
  5423.6 699.1 %while.158 = (s32[]{:T(128)}, f32[1024,512]{1,0:T(8,128)S(1)}, s32[]{:T(128)}, s32[]{:T(128)}, pred[]{:T(512)}, /*index=5*/s32[]{:T(128)}, s32[]{:T(128)}, s32[]...) while((s32[]{:T(128)}, f32[1024,512]{1,0:T(8,128)S(1)}, ...), condition=%wide.region_36.38_spmd.clone.clone, body=%wide.region_32.37_spmd.clone.clone.sunk | while | flops 337346784 | bytes 12650374 | solution.py:78
  5639.0 27.5 all-reduce.63.cloned.1.call-done
  5988.5 27.5 all-reduce.63.cloned.1.call-done
  6124.2 687.1 %while.159 = (s32[]{:T(128)}, f32[512,256]{1,0:T(8,128)S(1)}, s32[]{:T(128)}, s32[]{:T(128)}, pred[]{:T(512)}, /*index=5*/s32[]{:T(128)}, s32[]{:T(128)}, s32[]{...) while((s32[]{:T(128)}, f32[512,256]{1,0:T(8,128)S(1)}, ...), condition=%wide.region_41.43_spmd.clone.clone, body=%wide.region_37.42_spmd.clone.clone.sunk | while | flops 135168192 | bytes 6031206 | solution.py:78
  (1645 shorter events, 5644.5 us)
Async XLA Ops:
  45.6 64.5 all-reduce.27.cloned.1.call-start
  80.0 55.6 all-reduce.29.cloned.1.call-start
  176.8 61.7 all-reduce.27.cloned.1.call-start
  207.5 56.3 all-reduce.29.cloned.1.call-start
  304.9 62.5 all-reduce.27.cloned.1.call-start
  335.6 57.2 all-reduce.29.cloned.1.call-start
  434.0 61.7 all-reduce.27.cloned.1.call-start
  464.7 56.2 all-reduce.29.cloned.1.call-start
  562.1 61.7 all-reduce.27.cloned.1.call-start
  593.7 55.4 all-reduce.29.cloned.1.call-start
  690.2 61.7 all-reduce.27.cloned.1.call-start
  721.0 56.2 all-reduce.29.cloned.1.call-start
  818.4 62.6 all-reduce.27.cloned.1.call-start
  849.1 57.3 all-reduce.29.cloned.1.call-start
  947.5 61.7 all-reduce.27.cloned.1.call-start
  978.2 56.2 all-reduce.29.cloned.1.call-start
  1093.4 60.5 all-reduce.33.cloned.1.call-start
  1214.1 60.5 all-reduce.33.cloned.1.call-start
  1334.9 61.3 all-reduce.33.cloned.1.call-start
  1456.4 60.5 all-reduce.33.cloned.1.call-start
  1577.2 60.5 all-reduce.33.cloned.1.call-start
  1697.9 60.5 all-reduce.33.cloned.1.call-start
  1818.8 61.4 all-reduce.33.cloned.1.call-start
  1940.4 60.5 all-reduce.33.cloned.1.call-start
  2095.1 57.4 all-reduce.39.cloned.1.call-start
  2206.4 57.4 all-reduce.39.cloned.1.call-start
  2317.9 58.3 all-reduce.39.cloned.1.call-start
  2430.2 57.4 all-reduce.39.cloned.1.call-start
  2541.6 57.4 all-reduce.39.cloned.1.call-start
  2652.9 57.4 all-reduce.39.cloned.1.call-start
  2764.2 58.3 all-reduce.39.cloned.1.call-start
  2876.5 57.4 all-reduce.39.cloned.1.call-start
  3011.0 56.0 all-reduce.45.cloned.1.call-start
  3115.7 56.0 all-reduce.45.cloned.1.call-start
  3220.4 56.8 all-reduce.45.cloned.1.call-start
  3325.9 56.0 all-reduce.45.cloned.1.call-start
  3430.4 56.0 all-reduce.45.cloned.1.call-start
  3534.9 56.0 all-reduce.45.cloned.1.call-start
  3639.5 56.8 all-reduce.45.cloned.1.call-start
  3744.9 56.0 all-reduce.45.cloned.1.call-start
  3868.6 55.2 all-reduce.51.cloned.1.call-start
  3967.4 55.2 all-reduce.51.cloned.1.call-start
  4066.4 56.0 all-reduce.51.cloned.1.call-start
  4166.1 55.2 all-reduce.51.cloned.1.call-start
  4265.1 55.2 all-reduce.51.cloned.1.call-start
  4364.1 55.2 all-reduce.51.cloned.1.call-start
  4463.2 56.0 all-reduce.51.cloned.1.call-start
  4562.8 55.2 all-reduce.51.cloned.1.call-start
  (144 other events, 5972.4 us)
Sparse Core Ops, SparseCore 0:
  80.1 29.9 all-reduce.26
  207.6 30.8 all-reduce.26
  335.7 31.6 all-reduce.26
  464.8 30.7 all-reduce.26
  593.8 29.9 all-reduce.26
  721.1 30.7 all-reduce.26
  849.2 31.6 all-reduce.26
  978.4 30.7 all-reduce.26
  1124.5 29.3 all-reduce.32
  1244.4 30.1 all-reduce.32
  1365.2 30.9 all-reduce.32
  1486.8 30.1 all-reduce.32
  1608.3 29.3 all-reduce.32
  1728.3 30.1 all-reduce.32
  1849.2 30.9 all-reduce.32
  1970.8 30.1 all-reduce.32
  2124.0 28.5 all-reduce.38
  2234.5 29.3 all-reduce.38
  2345.9 30.2 all-reduce.38
  2458.2 29.3 all-reduce.38
  2570.5 28.5 all-reduce.38
  2680.9 29.3 all-reduce.38
  2792.2 30.2 all-reduce.38
  2904.5 29.3 all-reduce.38
  3039.6 27.3 all-reduce.44
  3143.4 28.2 all-reduce.44
  3248.1 29.0 all-reduce.44
  3353.6 28.2 all-reduce.44
  3459.0 27.3 all-reduce.44
  3562.6 28.1 all-reduce.44
  3667.2 29.0 all-reduce.44
  3772.6 28.1 all-reduce.44
  3994.9 27.7 all-reduce.50
  4093.9 28.5 all-reduce.50
  4193.6 27.7 all-reduce.50
  4391.6 27.7 all-reduce.50
  4490.6 28.5 all-reduce.50
  4590.3 27.7 all-reduce.50
  4797.0 27.0 all-reduce.56
  4891.5 27.8 all-reduce.56
  4987.0 27.0 all-reduce.56
  5175.8 27.0 all-reduce.56
  5270.4 27.8 all-reduce.56
  5365.7 27.0 all-reduce.56
  5639.1 27.4 all-reduce.62
  5988.6 27.4 all-reduce.62
  6336.7 26.9 all-reduce.68
  6680.0 26.9 all-reduce.68
  (144 shorter events, 2581.0 us)
where the time goes:
time: 6860 us; the launch traced here: 6840 us
  waiting for transfers between devices  3870 us (56%)
  other arithmetic  1820 us (27%)
  matrix products  821 us (12%)
  local copies, waits for them, and re-layouts  304 us (4%)
    psum x64, waiting for transfers between devices, panel_step(): lax.psum(jnp.where(below_mask & own_col, solved_blocks, 0.0).astype(jnp.b...  1820 us
    psum x64, waiting for transfers between devices, transposed_panel(): return lax.psum(spread, 'row')  1160 us
    psum x64, waiting for transfers between devices, panel_step(): diag_fac = lax.psum(jnp.where(is_owner, diag_own, 0.0), 'row')  896 us
    another operation x192, other arithmetic, panel_step(): jnp.linalg.cholesky(jnp.where(is_owner, diag_blk, eye_blk))  796 us
    dot_general x64, matrix products, panel_step(): lax.dot_general(row_panel.reshape(win_rows, blk_size), col_panel.reshape(...  716 us
    another operation x128, other arithmetic, panel_step(): lax.linalg.triangular_solve(diag_fac, col_blk, left_side=False, lower=Tru...  642 us
  transfers between devices with their start and end apart: 192, of which 192 were waited for; matrix products, arithmetic and copies ran while one was open for 2% of the time, Pallas kernels for 0%

commit v1 on v0

v1 whole, which is shorter than its diff:
```python
import jax
import jax.numpy as jnp
from jax import lax
from jax.experimental import pallas as pl
from jax.experimental.pallas import tpu as pltpu
from jax.sharding import PartitionSpec as P

NB = 64
BS = 128
ROWB = 32
COLB = 16
CHB = 4
NCH = ROWB // CHB
F32 = jnp.float32
BF16 = jnp.bfloat16
HI = lax.Precision.HIGHEST


def dot_nt(a, b, precision=None):
    return lax.dot_general(a, b, (((1,), (1,)), ((), ())), precision=precision, preferred_element_type=F32)


def factor_block(src_ref, g_ref):
    g_ref[...] = src_ref[...]
    for sb in range(4):
        lo = 32 * sb
        part = g_ref[lo:lo + 32, :]
        done_rows = []
        for tb in range(4):
            base = lo + 8 * tb
            rows = part.shape[0]
            lane = lax.broadcasted_iota(jnp.int32, (rows, BS), 1)
            row = lax.broadcasted_iota(jnp.int32, (rows, BS), 0)
            lane8 = lane[0:8]
            row8 = row[0:8]
            cols = [jnp.broadcast_to(part[:, base + q:base + q + 1], (rows, BS)) for q in range(8)]
            scale = jnp.zeros((8, BS), F32)
            for i in range(8):
                piv = jnp.broadcast_to(cols[i][i:i + 1, :], (8, BS))
                rs = lax.rsqrt(piv)
                inv = rs * rs
                scale = jnp.where(row8 == i, rs, scale)
                prow = jnp.broadcast_to(part[i:i + 1, :], (8, BS))
                nrow = jnp.where(lane8 == base + i, inv, prow * inv)
                mult = [jnp.where(row8 > i, cols[i][0:8], 0.0)] + [cols[i][8 * v:8 * v + 8] for v in range(1, rows // 8)]
                hit = [(lane8 == base + i) & (row8 > i)] + [lane8 == base + i] * (rows // 8 - 1)
                part = jnp.concatenate(
                    [jnp.where(hit[v], 0.0, part[8 * v:8 * v + 8]) - mult[v] * nrow for v in range(rows // 8)], axis=0)
                for q in range(i + 1, 8):
                    cq = cols[q]
                    t = jnp.broadcast_to(cq[i:i + 1, :], (8, BS)) * inv
                    cols[q] = jnp.concatenate(
                        [cq[8 * v:8 * v + 8] - mult[v] * t for v in range(rows // 8)], axis=0)
            done_rows.append(jnp.where(lane8 == row8 + base, 1.0, part[0:8]) * scale)
            if tb < 3:
                part = part[8:]
        panel = jnp.concatenate(done_rows, axis=0)
        g_ref[lo:lo + 32, :] = panel
        if sb < 3:
            lane = lax.broadcasted_iota(jnp.int32, (32, BS), 1)
            row = lax.broadcasted_iota(jnp.int32, (32, BS), 0)
            clean = jnp.where((lane < lo + 32) & (lane > row + lo), 0.0, panel)
            upd = lax.dot_general(panel, clean, (((0,), (0,)), ((), ())), precision=HI, preferred_element_type=F32)
            lane = lax.broadcasted_iota(jnp.int32, (96 - lo, BS), 1)
            keep = (lane < lo) | (lane >= lo + 32)
            g_ref[lo + 32:, :] = jnp.where(keep, g_ref[lo + 32:, :], 0.0) - upd[lo + 32:, :]


def kernel(a_hbm, o_hbm, mat, pan, g_ref, ch_d, ch_e, ch_f, ch_r, b1, b2, b1p, b2p,
           in_s, in_b, linv_in, stage,
           ld_sem, out_sem, rrow, rcol, s_src, s_fwd, in_s_sem, in_b_sem, st_sem, bst_sem,
           l_recv, l_send, done, init_recv, init_send):
    r = lax.axis_index("row")
    c = lax.axis_index("col")
    is_chain = (r == 0) & (c == 0)
    xc = c // 2

    bar = pltpu.get_barrier_semaphore()
    for rr in range(2):
        for cc in range(4):
            @pl.when((r != rr) | (c != cc))
            def _(rr=rr, cc=cc):
                pl.semaphore_signal(bar, inc=1, device_id={"row": rr, "col": cc}, device_id_type=pl.DeviceIdType.MESH)
    pl.semaphore_wait(bar, 7)

    def remote(src, dst, ssem, rsem, rr, cc):
        return pltpu.make_async_remote_copy(src_ref=src, dst_ref=dst, send_sem=ssem, recv_sem=rsem,
                                            device_id={"row": rr, "col": cc},
                                            device_id_type=pl.DeviceIdType.MESH)

    def load_col(s):
        return pltpu.make_async_copy(a_hbm.at[:, :, pl.ds(s * BS, BS)], mat.at[s], ld_sem.at[s])

    def out_col(s):
        off = pl.multiple_of(s * BS, BS)
        return pltpu.make_async_copy(mat.at[s], o_hbm.at[:, :, pl.ds(off, BS)], out_sem.at[s])

    for s in range(COLB):
        load_col(s).start()
    pan[2] = jnp.zeros(pan.shape[1:], BF16)
    for s in range(COLB):
        load_col(s).wait()

    init = [((0, 0), ch_d, None), ((1, 0), ch_e, None), ((1, 1), ch_f, None),
            ((2, 0), ch_r, 0), ((2, 1), ch_r, 1), ((2, 2), ch_r, 2)]
    for n, ((bi, bj), buf, sub) in enumerate(init):
        dst = buf if sub is None else buf.at[sub]
        own = (bi % 2, bj % 4)
        src = mat.at[bj // 4, bi // 2]
        if own == (0, 0):
            @pl.when(is_chain)
            def _(dst=dst, src=src):
                dst[...] = src[...]
        else:
            cp = remote(src, dst, init_send.at[n], init_recv.at[n], 0, 0)

            @pl.when((r == own[0]) & (c == own[1]))
            def _(cp=cp):
                cp.start()
                cp.wait_send()

            @pl.when(is_chain)
            def _(cp=cp):
                cp.wait_recv()

    def first_chunk(k, par):
        return ((k + 2 - par) // 2) // CHB

    def col_block(buf, s):
        idx = jnp.where(r == c % 2, 2 * s + xc, ROWB + s)
        return pan[buf, idx // 2, idx % 2]

    def row_copy(buf, q, ssem, rr, cc):
        return remote(pan.at[buf, pl.ds(2 * q, 2)], pan.at[buf, pl.ds(2 * q, 2)], ssem, rrow.at[buf, q], rr, cc)

    def col_copy(buf, q, half, ssem, rr, cc):
        return remote(pan.at[buf, pl.ds(2 * q, 2), half], pan.at[buf, COLB + q], ssem, rcol.at[buf, q], rr, cc)

    def step(k, carry):
        buf = lax.rem(k, 3)
        pbuf = lax.rem(k + 2, 3)
        ck = lax.rem(k, 4)
        cp_ = lax.rem(k + 3, 4)
        slot4 = lax.rem(k, 4)
        pslot4 = lax.rem(k + 3, 4)
        lslot = lax.rem(k // 4, 2)
        own_col = c == ck
        sk = k // 4

        def linv_copy(par):
            return remote(g_ref, linv_in.at[lslot], l_send.at[par], l_recv.at[lslot], par, ck)

        @pl.when(is_chain)
        def _():
            factor_block(ch_d, g_ref)

            @pl.when(ck == 0)
            def _():
                linv_in[lslot] = g_ref[...]

            @pl.when(ck != 0)
            def _():
                linv_copy(0).start()
            linv_copy(1).start()

            @pl.when(k < NB - 1)
            def _():
                lane = lax.broadcasted_iota(jnp.int32, (BS, BS), 1)
                row = lax.broadcasted_iota(jnp.int32, (BS, BS), 0)
                linv = jnp.where(lane <= row, g_ref[...], 0.0)
                x1 = dot_nt(ch_e[...], linv, HI).astype(BF16)
                b1[...] = x1
                ch_d[...] = ch_f[...] - dot_nt(x1, x1)

        pk = k - 1
        src_prev = c == cp_
        fwd_prev = (c % 2 == 1) & (xc != cp_ // 2) & (k > 0)
        q_row = first_chunk(pk, r)
        q_col = first_chunk(pk, 1 - r)

        @pl.when(k > 0)
        def _():
            def take(q, _):
                @pl.when(jnp.logical_not(src_prev))
                def _():
                    row_copy(pbuf, q, s_fwd.at[0, q], r, c).wait_recv()

                @pl.when(fwd_prev)
                def _():
                    row_copy(pbuf, q, s_fwd.at[0, q], r, c - 1).start()
                    col_copy(pbuf, q, xc, s_fwd.at[1, q], 1 - r, 2 * xc + r).start()
                return 0
            lax.fori_loop(q_row, NCH, take, 0)

            @pl.when(r != c % 2)
            def _():
                def take_col(q, _):
                    col_copy(pbuf, q, xc, s_fwd.at[1, q], 1 - r, c).wait_recv()
                    return 0
                lax.fori_loop(q_col, NCH, take_col, 0)

        row3 = k + 3
        t3 = row3 // 2
        b_copy = remote(pan.at[buf, t3 // 2, t3 % 2], in_b.at[slot4], bst_sem, in_b_sem.at[slot4], 0, 0)
        send_b = own_col & (row3 < NB) & (r == row3 % 2)

        @pl.when(own_col)
        def _():
            @pl.when(jnp.logical_not(is_chain))
            def _():
                linv_copy(r).wait_recv()

            @pl.when(k >= 3)
            def _():
                pl.semaphore_wait(done.at[lslot], 7)
            q0 = first_chunk(k, r)
            t0 = (k + 2 - r) // 2

            def clear(q, _):
                mat[sk, pl.ds(CHB * q, CHB)] = jnp.zeros((CHB, BS, BS), F32)
                return 0
            lax.fori_loop(0, q0, clear, 0)

            lane = lax.broadcasted_iota(jnp.int32, (BS, BS), 1)
            row = lax.broadcasted_iota(jnp.int32, (BS, BS), 0)

            def solve(q, _):
                linv = jnp.where(lane <= row, linv_in[lslot], 0.0)
                left = pan[pbuf, pl.ds(2 * q, 2)].reshape(CHB * BS, BS)
                cur = mat[sk, pl.ds(CHB * q, CHB)].reshape(CHB * BS, BS) - dot_nt(left, col_block(pbuf, sk))
                x = dot_nt(cur, linv, HI)
                rowid = lax.broadcasted_iota(jnp.int32, (CHB * BS, BS), 0)
                x = jnp.where(rowid >= (t0 - CHB * q) * BS, x, 0.0)
                mat[sk, pl.ds(CHB * q, CHB)] = x.reshape(CHB, BS, BS)
                pan[buf, pl.ds(2 * q, 2)] = x.astype(BF16).reshape(2, 2, BS, BS)
                row_copy(buf, q, s_src.at[0, q], r, 2 * xc + (1 - c % 2)).start()
                row_copy(buf, q, s_src.at[1, q], r, 2 * (1 - xc) + 1).start()
                col_copy(buf, q, xc, s_src.at[2, q], 1 - r, 2 * xc + r).start()

                @pl.when(send_b & (q == t3 // CHB))
                def _():
                    @pl.when(is_chain)
                    def _():
                        in_b[slot4] = pan[buf, t3 // 2, t3 % 2]

                    @pl.when(jnp.logical_not(is_chain))
                    def _():
                        b_copy.start()
                return 0
            lax.fori_loop(q0, NCH, solve, 0)

            @pl.when(r == k % 2)
            def _():
                g = linv_in[lslot]
                up = jnp.where(lane > row, g, jnp.where(lane == row, 1.0 / g, 0.0))
                mat[sk, k // 2] = up.T
            out_col(sk).start()

        m = lax.rem(c - k + 64, 4)
        send_s = (row3 < NB) & (r == row3 % 2) & (m != 0)
        msl = jnp.maximum(m - 1, 0)
        s_copy = remote(stage, in_s.at[slot4, msl], st_sem, in_s_sem.at[slot4, msl], 0, 0)

        @pl.when(send_s)
        def _():
            sm = (k + m) // 4
            val = mat[sm, t3] - dot_nt(pan[pbuf, t3 // 2, t3 % 2], col_block(pbuf, sm))

            @pl.when(is_chain)
            def _():
                in_s[slot4, msl] = val

            @pl.when(jnp.logical_not(is_chain))
            def _():
                stage[...] = val
                s_copy.start()

        @pl.when(k > 0)
        def _():
            s_lo = (k - c + 4) // 4

            def chunk(q, cols_, right):
                left = pan[pbuf, pl.ds(2 * q, 2)].reshape(CHB * BS, BS)
                u = dot_nt(left, right)
                for n, s in enumerate(cols_):
                    un = u[:, n * BS:(n + 1) * BS].reshape(CHB, BS, BS)
                    mat[s, pl.ds(CHB * q, CHB)] = mat[s, pl.ds(CHB * q, CHB)] - un

            def low_chunk(s):
                return ((4 * s + c - r + 1) // 2) // CHB

            @pl.when((s_lo % 2 == 1) & (s_lo < COLB))
            def _():
                def body(q, _):
                    chunk(q, (s_lo,), col_block(pbuf, s_lo))
                    return 0
                lax.fori_loop(low_chunk(s_lo), NCH, body, 0)

            def pair(sp, _):
                s0 = 2 * sp

                def body(q, _):
                    right = jnp.concatenate([col_block(pbuf, s0), col_block(pbuf, s0 + 1)], axis=0)
                    chunk(q, (s0, s0 + 1), right)
                    return 0
                lax.fori_loop(low_chunk(s0), NCH, body, 0)
                return 0
            lax.fori_loop((s_lo + 1) // 2, COLB // 2, pair, 0)

        @pl.when(send_s & jnp.logical_not(is_chain))
        def _():
            s_copy.wait_send()

        @pl.when(send_b & jnp.logical_not(is_chain))
        def _():
            b_copy.wait_send()

        @pl.when(k > 0)
        def _():
            def drain(q, _):
                @pl.when(src_prev)
                def _():
                    row_copy(pbuf, q, s_src.at[0, q], r, c).wait_send()
                    row_copy(pbuf, q, s_src.at[1, q], r, c).wait_send()
                    col_copy(pbuf, q, xc, s_src.at[2, q], r, c).wait_send()

                @pl.when(fwd_prev)
                def _():
                    row_copy(pbuf, q, s_fwd.at[0, q], r, c).wait_send()
                    col_copy(pbuf, q, xc, s_fwd.at[1, q], r, c).wait_send()
                return 0
            lax.fori_loop(q_row, NCH, drain, 0)

        @pl.when((k >= 1) & (k + 2 < NB))
        def _():
            tc = lax.rem(k + 2, 4)
            nslot = lax.rem((k + 2) // 4, 2)
            for rr in range(2):
                @pl.when((r != rr) | (c != tc))
                def _(rr=rr):
                    pl.semaphore_signal(done.at[nslot], inc=1, device_id={"row": rr, "col": tc},
                                        device_id_type=pl.DeviceIdType.MESH)

        @pl.when(is_chain)
        def _():
            @pl.when((k > 0) & (k + 2 < NB))
            def _():
                rown = k + 2
                for mm in range(3):
                    ocol = lax.rem(k + mm, 4)

                    @pl.when((rown % 2 != 0) | (ocol != 0))
                    def _(mm=mm):
                        remote(stage, in_s.at[pslot4, mm], st_sem, in_s_sem.at[pslot4, mm], 0, 0).wait_recv()

                @pl.when((rown % 2 != 0) | (cp_ != 0))
                def _():
                    remote(in_b.at[pslot4], in_b.at[pslot4], bst_sem, in_b_sem.at[pslot4], 0, 0).wait_recv()
                bn = in_b[pslot4]
                ch_r[0] = in_s[pslot4, 0] - dot_nt(bn, b1p[...])
                ch_r[1] = in_s[pslot4, 1] - dot_nt(bn, b2p[...])
                ch_r[2] = in_s[pslot4, 2] - dot_nt(bn, bn)

            @pl.when(k + 2 < NB)
            def _():
                lane = lax.broadcasted_iota(jnp.int32, (BS, BS), 1)
                row = lax.broadcasted_iota(jnp.int32, (BS, BS), 0)
                linv = jnp.where(lane <= row, g_ref[...], 0.0)
                x2 = dot_nt(ch_r[0], linv, HI).astype(BF16)
                b2[...] = x2
                ch_e[...] = ch_r[1] - dot_nt(x2, b1[...])
                ch_f[...] = ch_r[2] - dot_nt(x2, x2)
                b1p[...] = b1[...]
                b2p[...] = x2

            @pl.when(ck != 0)
            def _():
                linv_copy(0).wait_send()
            linv_copy(1).wait_send()
        return carry

    lax.fori_loop(0, NB, step, 0)
    for s in range(COLB):
        out_col(s).wait()


def solution(mesh):
    blk = lambda *shape: pltpu.VMEM(shape + (BS, BS), F32)
    bb = lambda *shape: pltpu.VMEM(shape + (BS, BS), BF16)
    dma = pltpu.SemaphoreType.DMA
    call = pl.pallas_call(
        kernel,
        out_shape=jax.ShapeDtypeStruct((ROWB, BS, COLB * BS), F32),
        in_specs=[pl.BlockSpec(memory_space=pl.ANY)],
        out_specs=pl.BlockSpec(memory_space=pl.ANY),
        scratch_shapes=[
            blk(COLB, ROWB), bb(3, 24, 2), blk(), blk(), blk(), blk(), blk(3), bb(), bb(), bb(), bb(),
            blk(4, 3), bb(4), blk(2), blk(),
            dma((COLB,)), dma((COLB,)), dma((3, NCH)), dma((3, NCH)), dma((3, NCH)), dma((2, NCH)),
            dma((4, 3)), dma((4,)), dma(()), dma(()),
            dma((2,)), dma((2,)), pltpu.SemaphoreType.REGULAR((2,)), dma((6,)), dma((6,)),
        ],
        compiler_params=pltpu.CompilerParams(collective_id=0, has_side_effects=True, vmem_limit_bytes=60 * 1024 * 1024),
        name="chol",
    )
    spec = P(("batch", "row"), None, "col")
    return jax.shard_map(lambda a: call(a), mesh=mesh, in_specs=(spec,), out_specs=spec, check_vma=False)
```

time: 6860 us -> 795 us (0.12)
  waiting for transfers between devices: 3870 us -> 0 us
  other arithmetic: 1820 us -> 0 us
  matrix products: 821 us -> 0 us
  Pallas kernels: 0 us -> 771 us
  local copies, waits for them, and re-layouts: 304 us -> 23.2 us
    psum x192 -> x0, waiting for transfers between devices: 3870 us -> none  [the longest x64 1820 us: panel_step(): lax.psum(jnp.where(below_mask & own_col, solved_blocks, 0.0).astype(jnp.b...]
    another operation x320 -> x0, other arithmetic: 1440 us -> none  [the longest x192 796 us: panel_step(): jnp.linalg.cholesky(jnp.where(is_owner, diag_blk, eye_blk))]
    pallas_call x0 -> x1, Pallas kernels: none -> 771 us  [solution(): call(a)]
    dot_general x64 -> x0, matrix products: 716 us -> none  [panel_step(): lax.dot_general(row_panel.reshape(win_rows, blk_size), col_panel.reshape(...]
    select_n x193 -> x0, other arithmetic: 263 us -> none  [the longest x64 109 us: transposed_panel(): jnp.where(row_id == col_id % row_devs, chosen, jnp.zeros_like(chosen))]
    dynamic_update_slice x71 -> x0, local copies, waits for them, and re-layouts: 120 us -> none  [the longest x64 62 us: panel_step(): window = lax.dynamic_update_slice_in_dim(window, new_col, col_off, axis=1)]
    another operation x64 -> x0, matrix products: 105 us -> none  [panel_step(): lax.linalg.triangular_solve(diag_fac, col_blk, left_side=False, lower=Tru...]
    dynamic_slice x64 -> x0, local copies, waits for them, and re-layouts: 92 us -> none  [panel_step(): col_blk = lax.dynamic_slice_in_dim(window, col_off, blk_size, axis=1)]
  transfers between devices with their start and end apart: 192 -> 0, of which waited for: 192 -> 0; matrix products, arithmetic and copies ran while one was open for 2% -> 0% of each run, Pallas kernels for 0% -> 0%
where the time goes in v1:
time: 795 us; the launch traced here: 794 us
  Pallas kernels  771 us (97%)
  local copies, waits for them, and re-layouts  23.2 us (3%)
    pallas_call x1, Pallas kernels, solution(): call(a)  771 us
    unnamed x1, local copies, waits for them, and re-layouts  23.2 us

profile of v1, /device:TPU:0, one launch (start us, length us, event | category | flops | bytes accessed | tf_op | source)
XLA Modules:
  0.0 793.7 jit_solution(88047024944094023)
XLA Ops:
  0.0 770.5 %chol.1 = f32[32,128,2048]{2,1,0:T(8,128)} custom-call(f32[32,128,2048]{2,1,0:T(8,128)} %a_hbm.1), custom_call_target="tpu_custom_call" | custom-call | tf_op jit(solution)/shard_map/chol/pallas_call | solution.py:407
  770.5 23.2 %copy.3 = f32[32,128,2048]{2,1,0:T(8,128)} copy(f32[32,128,2048]{2,1,0:T(8,128)} %chol.1) | data formatting | bytes 67108864

commit v2 on v1

--- a/solution.py
+++ b/solution.py
@@ -9,8 +9,10 @@
 BS = 128
 ROWB = 32
 COLB = 16
-CHB = 4
+CHB = 2
 NCH = ROWB // CHB
+DCB = 4
+NBUF = 5
 F32 = jnp.float32
 BF16 = jnp.bfloat16
 HI = lax.Precision.HIGHEST
@@ -97,7 +99,8 @@
 
     for s in range(COLB):
         load_col(s).start()
-    pan[2] = jnp.zeros(pan.shape[1:], BF16)
+    pan[NBUF - 1] = jnp.zeros(pan.shape[1:], BF16)
+    pan[NBUF - 2] = jnp.zeros(pan.shape[1:], BF16)
     for s in range(COLB):
         load_col(s).wait()
 
@@ -131,14 +134,38 @@
         return pan[buf, idx // 2, idx % 2]
 
     def row_copy(buf, q, ssem, rr, cc):
-        return remote(pan.at[buf, pl.ds(2 * q, 2)], pan.at[buf, pl.ds(2 * q, 2)], ssem, rrow.at[buf, q], rr, cc)
+        return remote(pan.at[buf, q], pan.at[buf, q], ssem, rrow.at[buf, q], rr, cc)
 
     def col_copy(buf, q, half, ssem, rr, cc):
-        return remote(pan.at[buf, pl.ds(2 * q, 2), half], pan.at[buf, COLB + q], ssem, rcol.at[buf, q], rr, cc)
+        return remote(pan.at[buf, q, half], pan.at[buf, COLB + q // 2, q % 2], ssem, rcol.at[buf, q], rr, cc)
+
+    def drain_panel(p):
+        b = lax.rem(p, NBUF)
+        cs = lax.rem(p, 4)
+
+        def body(q, _):
+            @pl.when(c == cs)
+            def _():
+                row_copy(b, q, s_src.at[b, 0, q], r, c).wait_send()
+                row_copy(b, q, s_src.at[b, 1, q], r, c).wait_send()
+                col_copy(b, q, xc, s_src.at[b, 2, q], r, c).wait_send()
+
+                @pl.when(q < first_chunk(p, r) + 2)
+                def _():
+                    row_copy(b, q, s_src.at[b, 3, q], r, c).wait_send()
+                    col_copy(b, q, xc, s_src.at[b, 4, q], r, c).wait_send()
+
+            @pl.when((c % 2 == 1) & (xc != cs // 2) & (q >= first_chunk(p, r) + 2))
+            def _():
+                row_copy(b, q, s_fwd.at[b, 0, q], r, c).wait_send()
+                col_copy(b, q, xc, s_fwd.at[b, 1, q], r, c).wait_send()
+            return 0
+        lax.fori_loop(first_chunk(p, r), NCH, body, 0)
 
     def step(k, carry):
-        buf = lax.rem(k, 3)
-        pbuf = lax.rem(k + 2, 3)
+        buf = lax.rem(k, NBUF)
+        pbuf = lax.rem(k + NBUF - 1, NBUF)
+        obuf = lax.rem(k + NBUF - 2, NBUF)
         ck = lax.rem(k, 4)
         cp_ = lax.rem(k + 3, 4)
         slot4 = lax.rem(k, 4)
@@ -177,27 +204,44 @@
         fwd_prev = (c % 2 == 1) & (xc != cp_ // 2) & (k > 0)
         q_row = first_chunk(pk, r)
         q_col = first_chunk(pk, 1 - r)
+        q_row2 = jnp.minimum(q_row + 2, NCH)
+        q_col2 = jnp.minimum(q_col + 2, NCH)
+
+        c2 = lax.rem(k + 2, 4)
+        late = (k > 1) & (c != c2) & (c != cp_) & jnp.logical_not((c % 2 == 1) & (xc != c2 // 2))
+        q_late = jnp.minimum(first_chunk(k - 2, r) + 2, NCH)
+
+        def take_late(q):
+            row_copy(obuf, q, s_fwd.at[obuf, 0, q], r, c).wait_recv()
+
+        def take_row(q):
+            @pl.when(jnp.logical_not(src_prev) & (k > 0))
+            def _():
+                row_copy(pbuf, q, s_fwd.at[pbuf, 0, q], r, c).wait_recv()
+
+            @pl.when(fwd_prev & (q >= q_row + 2))
+            def _():
+                row_copy(pbuf, q, s_fwd.at[pbuf, 0, q], r, c - 1).start()
+                col_copy(pbuf, q, xc, s_fwd.at[pbuf, 1, q], 1 - r, 2 * xc + r).start()
+
+        def take_rows(lo, hi):
+            def body(q, _):
+                take_row(q)
+                return 0
+            lax.fori_loop(lo, hi, body, 0)
+
+        def take_cols(b, lo, hi):
+            @pl.when(r != c % 2)
+            def _():
+                def body(q, _):
+                    col_copy(b, q, xc, s_fwd.at[b, 1, q], 1 - r, c).wait_recv()
+                    return 0
+                lax.fori_loop(lo, hi, body, 0)
 
         @pl.when(k > 0)
         def _():
-            def take(q, _):
-                @pl.when(jnp.logical_not(src_prev))
-                def _():
-                    row_copy(pbuf, q, s_fwd.at[0, q], r, c).wait_recv()
-
-                @pl.when(fwd_prev)
-                def _():
-                    row_copy(pbuf, q, s_fwd.at[0, q], r, c - 1).start()
-                    col_copy(pbuf, q, xc, s_fwd.at[1, q], 1 - r, 2 * xc + r).start()
-                return 0
-            lax.fori_loop(q_row, NCH, take, 0)
-
-            @pl.when(r != c % 2)
-            def _():
-                def take_col(q, _):
-                    col_copy(pbuf, q, xc, s_fwd.at[1, q], 1 - r, c).wait_recv()
-                    return 0
-                lax.fori_loop(q_col, NCH, take_col, 0)
+            take_cols(pbuf, q_col, jnp.minimum(q_col + 1, NCH))
+            take_rows(q_row, jnp.where(own_col, jnp.minimum(q_row + 1, NCH), q_row2))
 
         row3 = k + 3
         t3 = row3 // 2
@@ -210,7 +254,7 @@
             def _():
                 linv_copy(r).wait_recv()
 
-            @pl.when(k >= 3)
+            @pl.when(k >= NBUF - 2)
             def _():
                 pl.semaphore_wait(done.at[lslot], 7)
             q0 = first_chunk(k, r)
@@ -226,17 +270,22 @@
 
             def solve(q, _):
                 linv = jnp.where(lane <= row, linv_in[lslot], 0.0)
-                left = pan[pbuf, pl.ds(2 * q, 2)].reshape(CHB * BS, BS)
-                cur = mat[sk, pl.ds(CHB * q, CHB)].reshape(CHB * BS, BS) - dot_nt(left, col_block(pbuf, sk))
+                @pl.when((q > q_row) & (k > 0))
+                def _():
+                    take_row(q)
+
+                @pl.when(late & (q >= q_late))
+                def _():
+                    take_late(q)
+                left = jnp.concatenate([pan[obuf, q].reshape(CHB * BS, BS),
+                                        pan[pbuf, q].reshape(CHB * BS, BS)], axis=1)
+                right = jnp.concatenate([col_block(obuf, sk), col_block(pbuf, sk)], axis=1)
+                cur = mat[sk, pl.ds(CHB * q, CHB)].reshape(CHB * BS, BS) - dot_nt(left, right)
                 x = dot_nt(cur, linv, HI)
                 rowid = lax.broadcasted_iota(jnp.int32, (CHB * BS, BS), 0)
                 x = jnp.where(rowid >= (t0 - CHB * q) * BS, x, 0.0)
                 mat[sk, pl.ds(CHB * q, CHB)] = x.reshape(CHB, BS, BS)
-                pan[buf, pl.ds(2 * q, 2)] = x.astype(BF16).reshape(2, 2, BS, BS)
-                row_copy(buf, q, s_src.at[0, q], r, 2 * xc + (1 - c % 2)).start()
-                row_copy(buf, q, s_src.at[1, q], r, 2 * (1 - xc) + 1).start()
-                col_copy(buf, q, xc, s_src.at[2, q], 1 - r, 2 * xc + r).start()
-
+                pan[buf, q] = x.astype(BF16).reshape(CHB, BS, BS)
                 @pl.when(send_b & (q == t3 // CHB))
                 def _():
                     @pl.when(is_chain)
@@ -246,6 +295,15 @@
                     @pl.when(jnp.logical_not(is_chain))
                     def _():
                         b_copy.start()
+
+                row_copy(buf, q, s_src.at[buf, 0, q], r, 2 * xc + (1 - c % 2)).start()
+                row_copy(buf, q, s_src.at[buf, 1, q], r, 2 * (1 - xc) + 1).start()
+                col_copy(buf, q, xc, s_src.at[buf, 2, q], 1 - r, 2 * xc + r).start()
+
+                @pl.when(q < q0 + 2)
+                def _():
+                    row_copy(buf, q, s_src.at[buf, 3, q], r, 2 * (1 - xc)).start()
+                    col_copy(buf, q, 1 - xc, s_src.at[buf, 4, q], 1 - r, 2 * (1 - xc) + r).start()
                 return 0
             lax.fori_loop(q0, NCH, solve, 0)
 
@@ -256,6 +314,10 @@
                 mat[sk, k // 2] = up.T
             out_col(sk).start()
 
+        @pl.when(k > 0)
+        def _():
+            take_cols(pbuf, jnp.minimum(q_col + 1, NCH), q_col2)
+
         m = lax.rem(c - k + 64, 4)
         send_s = (row3 < NB) & (r == row3 % 2) & (m != 0)
         msl = jnp.maximum(m - 1, 0)
@@ -264,7 +326,9 @@
         @pl.when(send_s)
         def _():
             sm = (k + m) // 4
-            val = mat[sm, t3] - dot_nt(pan[pbuf, t3 // 2, t3 % 2], col_block(pbuf, sm))
+            left = jnp.concatenate([pan[obuf, t3 // 2, t3 % 2], pan[pbuf, t3 // 2, t3 % 2]], axis=1)
+            right = jnp.concatenate([col_block(obuf, sm), col_block(pbuf, sm)], axis=1)
+            val = mat[sm, t3] - dot_nt(left, right)
 
             @pl.when(is_chain)
             def _():
@@ -275,35 +339,50 @@
                 stage[...] = val
                 s_copy.start()
 
-        @pl.when(k > 0)
+        @pl.when(fwd_prev & jnp.logical_not(own_col))
+        def _():
+            take_rows(q_row2, NCH)
+
+        @pl.when(k > 1)
+        def _():
+            take_cols(obuf, jnp.minimum(first_chunk(k - 2, 1 - r) + 2, NCH), NCH)
+
+            @pl.when(late & jnp.logical_not(own_col))
+            def _():
+                def body(q, _):
+                    take_late(q)
+                    return 0
+                lax.fori_loop(q_late, NCH, body, 0)
+
+        @pl.when(k > 1)
         def _():
             s_lo = (k - c + 4) // 4
 
             def chunk(q, cols_, right):
-                left = pan[pbuf, pl.ds(2 * q, 2)].reshape(CHB * BS, BS)
+                left = pan[obuf, pl.ds(2 * q, 2)].reshape(DCB * BS, BS)
                 u = dot_nt(left, right)
                 for n, s in enumerate(cols_):
-                    un = u[:, n * BS:(n + 1) * BS].reshape(CHB, BS, BS)
-                    mat[s, pl.ds(CHB * q, CHB)] = mat[s, pl.ds(CHB * q, CHB)] - un
+                    un = u[:, n * BS:(n + 1) * BS].reshape(DCB, BS, BS)
+                    mat[s, pl.ds(DCB * q, DCB)] = mat[s, pl.ds(DCB * q, DCB)] - un
 
             def low_chunk(s):
-                return ((4 * s + c - r + 1) // 2) // CHB
+                return ((4 * s + c - r + 1) // 2) // DCB
 
             @pl.when((s_lo % 2 == 1) & (s_lo < COLB))
             def _():
                 def body(q, _):
-                    chunk(q, (s_lo,), col_block(pbuf, s_lo))
+                    chunk(q, (s_lo,), col_block(obuf, s_lo))
                     return 0
-                lax.fori_loop(low_chunk(s_lo), NCH, body, 0)
+                lax.fori_loop(low_chunk(s_lo), ROWB // DCB, body, 0)
 
             def pair(sp, _):
                 s0 = 2 * sp
 
                 def body(q, _):
-                    right = jnp.concatenate([col_block(pbuf, s0), col_block(pbuf, s0 + 1)], axis=0)
+                    right = jnp.concatenate([col_block(obuf, s0), col_block(obuf, s0 + 1)], axis=0)
                     chunk(q, (s0, s0 + 1), right)
                     return 0
-                lax.fori_loop(low_chunk(s0), NCH, body, 0)
+                lax.fori_loop(low_chunk(s0), ROWB // DCB, body, 0)
                 return 0
             lax.fori_loop((s_lo + 1) // 2, COLB // 2, pair, 0)
 
@@ -315,26 +394,14 @@
         def _():
             b_copy.wait_send()
 
-        @pl.when(k > 0)
-        def _():
-            def drain(q, _):
-                @pl.when(src_prev)
-                def _():
-                    row_copy(pbuf, q, s_src.at[0, q], r, c).wait_send()
-                    row_copy(pbuf, q, s_src.at[1, q], r, c).wait_send()
-                    col_copy(pbuf, q, xc, s_src.at[2, q], r, c).wait_send()
-
-                @pl.when(fwd_prev)
-                def _():
-                    row_copy(pbuf, q, s_fwd.at[0, q], r, c).wait_send()
-                    col_copy(pbuf, q, xc, s_fwd.at[1, q], r, c).wait_send()
-                return 0
-            lax.fori_loop(q_row, NCH, drain, 0)
-
-        @pl.when((k >= 1) & (k + 2 < NB))
-        def _():
-            tc = lax.rem(k + 2, 4)
-            nslot = lax.rem((k + 2) // 4, 2)
+        @pl.when(k > 1)
+        def _():
+            drain_panel(k - 2)
+
+        @pl.when(k - 2 + NBUF < NB)
+        def _():
+            tc = lax.rem(k - 2 + NBUF, 4)
+            nslot = lax.rem((k - 2 + NBUF) // 4, 2)
             for rr in range(2):
                 @pl.when((r != rr) | (c != tc))
                 def _(rr=rr):
@@ -380,6 +447,7 @@
         return carry
 
     lax.fori_loop(0, NB, step, 0)
+    drain_panel(jnp.int32(NB - 2))
     for s in range(COLB):
         out_col(s).wait()
 
@@ -394,9 +462,9 @@
         in_specs=[pl.BlockSpec(memory_space=pl.ANY)],
         out_specs=pl.BlockSpec(memory_space=pl.ANY),
         scratch_shapes=[
-            blk(COLB, ROWB), bb(3, 24, 2), blk(), blk(), blk(), blk(), blk(3), bb(), bb(), bb(), bb(),
+            blk(COLB, ROWB), bb(NBUF, 24, 2), blk(), blk(), blk(), blk(), blk(3), bb(), bb(), bb(), bb(),
             blk(4, 3), bb(4), blk(2), blk(),
-            dma((COLB,)), dma((COLB,)), dma((3, NCH)), dma((3, NCH)), dma((3, NCH)), dma((2, NCH)),
+            dma((COLB,)), dma((COLB,)), dma((NBUF, NCH)), dma((NBUF, NCH)), dma((NBUF, 5, NCH)), dma((NBUF, 2, NCH)),
             dma((4, 3)), dma((4,)), dma(()), dma(()),
             dma((2,)), dma((2,)), pltpu.SemaphoreType.REGULAR((2,)), dma((6,)), dma((6,)),
         ],

time: 795 us -> 722 us (0.908)
  Pallas kernels: 771 us -> 698 us
    pallas_call x1, Pallas kernels: 771 us -> 698 us  [solution(): call(a)]
where the time goes in v2:
time: 722 us; the launch traced here: 721 us
  Pallas kernels  698 us (97%)
  local copies, waits for them, and re-layouts  23.2 us (3%)
    pallas_call x1, Pallas kernels, solution(): call(a)  698 us
    unnamed x1, local copies, waits for them, and re-layouts  23.2 us

profile of v2, /device:TPU:0, one launch (start us, length us, event | category | flops | bytes accessed | tf_op | source)
XLA Modules:
  0.0 721.1 jit_solution(3196029882942307764)
XLA Ops:
  0.0 697.9 %chol.1 = f32[32,128,2048]{2,1,0:T(8,128)} custom-call(f32[32,128,2048]{2,1,0:T(8,128)} %a_hbm.1), custom_call_target="tpu_custom_call" | custom-call | tf_op jit(solution)/shard_map/chol/pallas_call | solution.py:475
  697.9 23.2 %copy.3 = f32[32,128,2048]{2,1,0:T(8,128)} copy(f32[32,128,2048]{2,1,0:T(8,128)} %chol.1) | data formatting | bytes 67108864
